TPU v7x, 8 devices: a whole 2x2x1 slice. The times are simulated.
8 devices in a mesh: data: 8 (over z, y, x, core).
Axes of the slice: x: 2, y: 2, z: 1, core: 2. Of those that a mesh axis runs over, the one named last changes fastest.
Arguments:
- x_in: bfloat16 [32768, 1024], P('data')
- dy_in: bfloat16 [32768, 1024], P('data')
- weights: bfloat16 [4, 1024, 1024], replicated
- a_old: float32 [4096, 1024], P('data')
- s_old: float32 [4096, 1024], P('data')
- a_inv: float32 [4096, 1024], P('data')
- s_inv: float32 [4, 1024, 1024], replicated
Outputs:
- output 1: float32 [4, 1024, 1024], replicated
- output 2: float32 [4096, 1024], P('data')
- output 3: float32 [4096, 1024], P('data')
All inputs are finite; a program needn't handle non-finite values.
Results may differ from a plain program's by a relative error of at most 0.001.
Values are sent between devices in bfloat16 or wider.
A program may use at most 1 GiB of HBM per device.

v0:
```python
import functools
import jax
import jax.numpy as jnp
from jax import lax
from jax.sharding import PartitionSpec as P

FACTOR_DECAY = 0.75
PRECISE = lax.Precision.HIGHEST


def gelu_grad(pre_act, d_act):
    pullback = jax.vjp(functools.partial(jax.nn.gelu, approximate=True), pre_act.astype(jnp.float32))[1]
    return pullback(d_act.astype(jnp.float32))[0].astype(jnp.bfloat16)


def cross_rows(left_op, right_op):
    return jnp.einsum("bi,bj->ij", left_op, right_op, preferred_element_type=jnp.float32)


def local_pass(x_loc, dy_loc, weights):
    n_layers = weights.shape[0]
    layer_inputs = [x_loc]
    pre_acts = []
    for layer_id in range(n_layers - 1):
        pre_act = jnp.dot(layer_inputs[layer_id], weights[layer_id], preferred_element_type=jnp.float32).astype(jnp.bfloat16)
        pre_acts.append(pre_act)
        layer_inputs.append(jax.nn.gelu(pre_act.astype(jnp.float32), approximate=True).astype(jnp.bfloat16))
    out_grads = [dy_loc] * n_layers
    for layer_id in range(n_layers - 1, 0, -1):
        d_act = jnp.einsum("bj,ij->bi", out_grads[layer_id], weights[layer_id], preferred_element_type=jnp.float32).astype(jnp.bfloat16)
        out_grads[layer_id - 1] = gelu_grad(pre_acts[layer_id - 1], d_act)
    return layer_inputs, out_grads


def solution(mesh):
    n_dev = mesh.shape["data"]

    def device_step(x_loc, dy_loc, weights, a_old_rows, s_old_rows, a_inv_rows, s_inv):
        n_layers = weights.shape[0]
        model_width = weights.shape[1]
        batch_total = x_loc.shape[0] * n_dev
        layer_inputs, out_grads = local_pass(x_loc, dy_loc, weights)
        a_loc = jnp.concatenate([cross_rows(h_in, h_in) for h_in in layer_inputs], axis=0) / batch_total
        s_loc = jnp.concatenate([cross_rows(g_out, g_out) for g_out in out_grads], axis=0) / batch_total
        w_loc = jnp.stack([cross_rows(h_in, g_out) for h_in, g_out in zip(layer_inputs, out_grads)]) / batch_total
        a_sum = lax.psum_scatter(a_loc, "data", scatter_dimension=0, tiled=True)
        s_sum = lax.psum_scatter(s_loc, "data", scatter_dimension=0, tiled=True)
        w_grad = lax.psum(w_loc, "data")
        own_rows = a_old_rows.shape[0]
        layer_id = (lax.axis_index("data") * own_rows) // model_width
        w_grad_own = lax.dynamic_index_in_dim(w_grad, layer_id, axis=0, keepdims=False)
        s_inv_own = lax.dynamic_index_in_dim(s_inv, layer_id, axis=0, keepdims=False)
        left_prod = jnp.dot(a_inv_rows, w_grad_own, precision=PRECISE)
        u_rows = jnp.dot(left_prod, s_inv_own, precision=PRECISE)
        u_full = lax.all_gather(u_rows, "data", axis=0, tiled=True).reshape(n_layers, model_width, model_width)
        a_new = FACTOR_DECAY * a_old_rows + (1.0 - FACTOR_DECAY) * a_sum
        s_new = FACTOR_DECAY * s_old_rows + (1.0 - FACTOR_DECAY) * s_sum
        return u_full, a_new, s_new

    row_spec = P("data", None)
    return jax.shard_map(
        device_step,
        mesh=mesh,
        in_specs=(row_spec, row_spec, P(), row_spec, row_spec, row_spec, P()),
        out_specs=(P(), row_spec, row_spec),
        check_vma=False,
    )
```

profile of v0, /device:TPU:0, one launch (start us, length us, event | category | flops | bytes accessed | tf_op | source)
XLA Modules:
  0.0 727.5 jit_solution(6107399124853479564)
XLA Ops:
  7.2 15.0 %convolution_convert_fusion.2 = bf16[4096,1024]{1,0:T(8,128)(2,1)} fusion(bf16[4096,1024]{1,0:T(8,128)(2,1)} %param.7, bf16[4,1024,1024]{2,1,0:T(8,128)(2,1)} %param.9), kind=kOutput, calls=%fused_computation.56 | convolution fusion | flops 8594128896 | bytes 18874368 | tf_op jit(solution)/shard_map/dot_general | solution.py:25
  22.3 15.6 %convolution_convert_fusion.1 = bf16[4096,1024]{1,0:T(8,128)(2,1)} fusion(bf16[4,1024,1024]{2,1,0:T(8,128)(2,1)S(1)} %copy-done.2, bf16[4096,1024]{1,0:T(8,128)(2,1)} %convolution_convert_fusion.2), kind=kOutput, calls=%fused_computation.55 | convolution fusion | flops 8636071936 | bytes 18874368 | tf_op jit(solution)/shard_map/dot_general | solution.py:25
  37.8 15.8 %convolution_convert_fusion = bf16[4096,1024]{1,0:T(8,128)(2,1)} fusion(bf16[4,1024,1024]{2,1,0:T(8,128)(2,1)S(1)} %copy-done.2, bf16[4096,1024]{1,0:T(8,128)(2,1)} %convolution_convert_fusion.1), kind=kOutput, calls=%fused_computation.54 | convolution fusion | flops 8636071936 | bytes 18874368 | tf_op jit(solution)/shard_map/dot_general | solution.py:25
  53.6 15.5 %convolution_bitcast_fusion = f32[1,1024,1024]{1,2,0:T(8,128)} fusion(bf16[4096,1024]{1,0:T(8,128)(2,1)} %param.8, bf16[4096,1024]{1,0:T(8,128)(2,1)} %convolution_convert_fusion), kind=kOutput, calls=%fused_computation.63 | convolution fusion | flops 8631877632 | bytes 20971520 | tf_op jit(solution)/shard_map/bi,bj->ij/dot_general | solution.py:17
  69.1 24.3 %fusion.5 = bf16[4096,1024]{1,0:T(8,128)(2,1)} fusion(bf16[4096,1024]{1,0:T(8,128)(2,1)} %convolution_convert_fusion, bf16[4096,1024]{1,0:T(8,128)(2,1)} %param.8, bf16[4,1024,1024]{2,1,0:T(8,128)(2,1)S(1)} %copy-done.2), kind=kOutput, calls=%fused_computation.23 | convolution fusion | flops 8686403584 | bytes 27262976 | tf_op jit(solution)/shard_map/bj,ij->bi/dot_general | solution.py:30
  93.4 14.1 %convolution_bitcast_fusion.1 = f32[1,1024,1024]{1,2,0:T(8,128)S(1)} fusion(bf16[4096,1024]{1,0:T(8,128)(2,1)} %fusion.5, bf16[4096,1024]{1,0:T(8,128)(2,1)} %convolution_convert_fusion.1), kind=kOutput, calls=%fused_computation.64 | convolution fusion | flops 8631877632 | bytes 20971520 | tf_op jit(solution)/shard_map/bi,bj->ij/dot_general | solution.py:17
  107.5 25.5 %fusion.8 = bf16[4096,1024]{1,0:T(8,128)(2,1)} fusion(bf16[4096,1024]{1,0:T(8,128)(2,1)} %convolution_convert_fusion.1, bf16[4096,1024]{1,0:T(8,128)(2,1)} %fusion.5, bf16[4,1024,1024]{2,1,0:T(8,128)(2,1)} %param.9), kind=kOutput, calls=%fused_computation.26 | convolution fusion | flops 8686403584 | bytes 27262976 | tf_op jit(solution)/shard_map/bj,ij->bi/dot_general | solution.py:30
  132.9 14.1 %convolution_bitcast_fusion.2 = f32[1,1024,1024]{1,2,0:T(8,128)S(1)} fusion(bf16[4096,1024]{1,0:T(8,128)(2,1)} %fusion.8, bf16[4096,1024]{1,0:T(8,128)(2,1)} %convolution_convert_fusion.2), kind=kOutput, calls=%fused_computation.65 | convolution fusion | flops 8631877632 | bytes 20971520 | tf_op jit(solution)/shard_map/bi,bj->ij/dot_general | solution.py:17
  147.0 25.3 %fusion.11 = bf16[4096,1024]{1,0:T(8,128)(2,1)} fusion(bf16[4096,1024]{1,0:T(8,128)(2,1)} %convolution_convert_fusion.2, bf16[4096,1024]{1,0:T(8,128)(2,1)} %fusion.8, bf16[4,1024,1024]{2,1,0:T(8,128)(2,1)} %param.9), kind=kOutput, calls=%fused_computation.29 | convolution fusion | flops 8686403584 | bytes 27262976 | tf_op jit(solution)/shard_map/bj,ij->bi/dot_general | solution.py:30
  172.3 13.4 %convolution_bitcast_fusion.3 = f32[1,1024,1024]{1,2,0:T(8,128)S(1)} fusion(bf16[4096,1024]{1,0:T(8,128)(2,1)} %fusion.11, bf16[4096,1024]{1,0:T(8,128)(2,1)} %param.7), kind=kOutput, calls=%fused_computation.66 | convolution fusion | flops 8589934592 | bytes 20971520 | tf_op jit(solution)/shard_map/bi,bj->ij/dot_general | solution.py:17
  192.1 15.8 %fusion.64 = f32[1024,1024]{1,0:T(8,128)S(1)} fusion(bf16[4096,1024]{1,0:T(8,128)(2,1)} %param.7), kind=kOutput, calls=%fused_computation.86 | convolution fusion | flops 8589934592 | bytes 12582912 | tf_op jit(solution)/shard_map/bi,bj->ij/dot_general | solution.py:17
  207.9 22.3 %fusion.60 = f32[1024,1024]{1,0:T(8,128)S(1)} fusion(bf16[4096,1024]{1,0:T(8,128)(2,1)} %convolution_convert_fusion.2), kind=kOutput, calls=%fused_computation.85 | convolution fusion | flops 8631877632 | bytes 12582912 | tf_op jit(solution)/shard_map/bi,bj->ij/dot_general | solution.py:17
  230.2 22.3 %fusion.56 = f32[1024,1024]{1,0:T(8,128)S(1)} fusion(bf16[4096,1024]{1,0:T(8,128)(2,1)} %convolution_convert_fusion.1), kind=kOutput, calls=%fused_computation.84 | convolution fusion | flops 8631877632 | bytes 12582912 | tf_op jit(solution)/shard_map/bi,bj->ij/dot_general | solution.py:17
  252.5 22.5 %fusion.53 = f32[1024,1024]{1,0:T(8,128)S(1)} fusion(bf16[4096,1024]{1,0:T(8,128)(2,1)} %convolution_convert_fusion), kind=kOutput, calls=%fused_computation.83 | convolution fusion | flops 8631877632 | bytes 12582912 | tf_op jit(solution)/shard_map/bi,bj->ij/dot_general | solution.py:17
  282.4 15.1 %fusion.68 = f32[1024,1024]{1,0:T(8,128)S(1)} fusion(bf16[4096,1024]{1,0:T(8,128)(2,1)} %param.8), kind=kOutput, calls=%fused_computation.90 | convolution fusion | flops 8589934592 | bytes 12582912 | tf_op jit(solution)/shard_map/bi,bj->ij/dot_general | solution.py:17
  297.5 15.2 %fusion.67 = f32[1024,1024]{1,0:T(8,128)S(1)} fusion(bf16[4096,1024]{1,0:T(8,128)(2,1)} %fusion.5), kind=kOutput, calls=%fused_computation.89 | convolution fusion | flops 8589934592 | bytes 12582912 | tf_op jit(solution)/shard_map/bi,bj->ij/dot_general | solution.py:17
  312.8 8.9 %fusion.66 = f32[1024,1024]{1,0:T(8,128)S(1)} fusion(bf16[4096,1024]{1,0:T(8,128)(2,1)S(1)} %bitcast.56), kind=kOutput, calls=%fused_computation.88 | convolution fusion | flops 8589934592 | bytes 12582912 | tf_op jit(solution)/shard_map/bi,bj->ij/dot_general | solution.py:17
  321.7 15.0 %fusion.65 = f32[1024,1024]{1,0:T(8,128)S(1)} fusion(bf16[4096,1024]{1,0:T(8,128)(2,1)} %fusion.11), kind=kOutput, calls=%fused_computation.87 | convolution fusion | flops 8589934592 | bytes 12582912 | tf_op jit(solution)/shard_map/bi,bj->ij/dot_general | solution.py:17
  344.2 57.2 %all-reduce.2.cloned.1.call-done = f32[4,1024,1024]{1,2,0:T(8,128)} async-done(((f32[4,1024,1024]{1,2,0:T(8,128)}), f32[4,1024,1024]{1,2,0:T(8,128)}) %all-reduce.2.cloned.1.call-update) | async-done | bytes 16777232 | tf_op jit(solution)/shard_map/psum | solution.py:48
  410.3 9.9 %fusion.33 = f32[512,1024]{1,0:T(8,128)} fusion(f32[1024,512]{1,0:T(8,128)S(1)} %fusion.35, f32[4,1024,1024]{2,1,0:T(8,128)} %param.13, s32[]{:T(128)S(6)} %select_n.11), kind=kOutput, calls=%fused_computation.57 | convolution fusion | flops 6442450944 | bytes 8388612 | tf_op jit(solution)/shard_map/dot_general | solution.py:54
  420.1 91.6 %reduce-scatter.3.cloned.1.call-done = f32[512,1024]{1,0:T(8,128)} async-done(((f32[4096,1024]{1,0:T(8,128)}), f32[512,1024]{1,0:T(8,128)}) %reduce-scatter.3.cloned.1.call-update) | async-done | bytes 2097168 | tf_op jit(solution)/shard_map/reduce_scatter | solution.py:46
  516.0 106.3 %reduce-scatter.5.cloned.1.call-done = f32[512,1024]{1,0:T(8,128)} async-done(((f32[4096,1024]{1,0:T(8,128)}), f32[512,1024]{1,0:T(8,128)}) %reduce-scatter.5.cloned.1.call-update) | async-done | bytes 2097168 | tf_op jit(solution)/shard_map/reduce_scatter | solution.py:47
  626.4 82.2 %all-gather.2.cloned.1.call-done = f32[4096,1024]{1,0:T(8,128)} async-done(((f32[512,1024]{1,0:T(8,128)}), f32[4096,1024]{1,0:T(8,128)}) %all-gather.2.cloned.1.call-update) | async-done | bytes 16777232 | tf_op jit(solution)/shard_map/all_gather | solution.py:55
  708.6 12.0 %copy.18 = f32[4,1024,1024]{2,1,0:T(8,128)} copy(f32[4,1024,1024]{2,1,0:T(8,128)} %bitcast.54) | data formatting | bytes 33554432
  (25 shorter events, 38.5 us)
Async XLA Ops:
  7.2 394.2 %copy-start = (f32[512,1024]{1,0:T(8,128)S(1)}, f32[512,1024]{1,0:T(8,128)}, u32[]{:S(2)}) copy-start(f32[512,1024]{1,0:T(8,128)} %param.12) | copy-start | bytes 6291460
  7.2 394.1 %all-reduce.2.cloned.1.call-start = ((), (), s32[]{:S(2)}) async-start(), calls=%async_computation.2 | async-start | bytes 33554432 | tf_op jit(solution)/shard_map/psum | solution.py:48
  7.2 15.0 %copy-start.2 = (bf16[4,1024,1024]{2,1,0:T(8,128)(2,1)S(1)}, bf16[4,1024,1024]{2,1,0:T(8,128)(2,1)}, u32[]{:S(2)}) copy-start(bf16[4,1024,1024]{2,1,0:T(8,128)(2,1)} %param.9) | copy-start | bytes 25165828
  172.3 13.4 %copy-start.1 = (f32[1,1024,1024]{1,2,0:T(8,128)S(1)}, f32[1,1024,1024]{1,2,0:T(8,128)}, u32[]{:S(2)}) copy-start(f32[1,1024,1024]{1,2,0:T(8,128)} %convolution_bitcast_fusion) | copy-start | bytes 12582916
  192.1 319.7 %reduce-scatter.3.cloned.1.call-start = ((), (), s32[]{:S(2)}) async-start(), calls=%async_computation.4 | async-start | bytes 18874368 | tf_op jit(solution)/shard_map/reduce_scatter | solution.py:46
  282.3 339.9 %reduce-scatter.5.cloned.1.call-start = ((), (), s32[]{:S(2)}) async-start(), calls=%async_computation.5 | async-start | bytes 18874368 | tf_op jit(solution)/shard_map/reduce_scatter | solution.py:47
  282.4 30.4 %slice-start = ((s8[8388608]{0:T(1024)(128)(4,1)}), s8[4194304]{0:T(1024)(128)(4,1)S(1)}, s32[]{:S(2)}) async-start(s8[8388608]{0:T(1024)(128)(4,1)} %bitcast.55), calls=%async_computation.6 | async-start | bytes 8388608
  297.5 15.3 %slice-start.1 = ((s8[8388608]{0:T(1024)(128)(4,1)}), s8[4194304]{0:T(1024)(128)(4,1)S(1)}, s32[]{:S(2)}) async-start(s8[8388608]{0:T(1024)(128)(4,1)} %bitcast.55), calls=%async_computation.7 | async-start | bytes 8388608
  344.1 364.5 %all-gather.2.cloned.1.call-start = ((), (), s32[]{:S(2)}) async-start(), calls=%async_computation.3 | async-start | bytes 18874368 | tf_op jit(solution)/shard_map/all_gather | solution.py:55
Sparse Core Ops, SparseCore 0:
  192.2 209.0 all-reduce.1
  404.8 106.9 reduce-scatter.2
  515.3 106.9 reduce-scatter.4
  624.5 84.0 all-gather.1
where the time goes:
time: 735 us; the launch traced here: 728 us
  waiting for transfers between devices  337 us (46%)
  matrix products  334 us (45%)
  other arithmetic  29.3 us (4%)
  between operations  14.4 us (2%)
  local copies, waits for them, and re-layouts  12 us (2%)
    dot_general x12, matrix products, cross_rows(): jnp.einsum('bi,bj->ij', left_op, right_op, preferred_element_type=jnp.flo...  194 us
    reduce_scatter x1, waiting for transfers between devices, device_step(): s_sum = lax.psum_scatter(s_loc, 'data', scatter_dimension=0, tiled=True)  106 us
    reduce_scatter x1, waiting for transfers between devices, device_step(): a_sum = lax.psum_scatter(a_loc, 'data', scatter_dimension=0, tiled=True)  91.6 us
    all_gather x1, waiting for transfers between devices, device_step(): lax.all_gather(u_rows, 'data', axis=0, tiled=True)  82.2 us
    dot_general x3, matrix products, local_pass(): jnp.einsum('bj,ij->bi', out_grads[layer_id], weights[layer_id], preferred...  75 us
    psum x1, waiting for transfers between devices, device_step(): w_grad = lax.psum(w_loc, 'data')  57.2 us
    dot_general x3, matrix products, local_pass(): jnp.dot(layer_inputs[layer_id], weights[layer_id], preferred_element_type...  46.4 us
  transfers between devices with their start and end apart: 4, of which 4 were waited for; matrix products, arithmetic and copies ran while one was open for 25% of the time, Pallas kernels for 0%

commit v1 on v0

v1 whole, which is shorter than its diff:
```python
import functools
import math
import jax
import jax.numpy as jnp
from jax import lax
from jax.experimental import pallas as pl
from jax.experimental.pallas import tpu as pltpu
from jax.sharding import PartitionSpec as P

F32 = jnp.float32
BF16 = jnp.bfloat16
MESH = pl.DeviceIdType.MESH
PRECISE = lax.Precision.HIGHEST
FACTOR_DECAY = 0.75
GELU_A = math.sqrt(2.0 / math.pi)
GELU_B = GELU_A * 0.044715

D = 1024
BK = 512
HALF = D // 2
PR, PC = 256, 1280


def gelu(z):
    hz = 0.5 * z
    return hz + hz * jnp.tanh(z * (GELU_A + GELU_B * (z * z)))


def gelu_slope(z):
    m = GELU_B * (z * z)
    t = jnp.tanh(z * (GELU_A + m))
    return (0.5 + 0.5 * t) + (0.5 * z) * (1.0 - t * t) * (GELU_A + 3.0 * m)


def rows_dot(a, b):
    return lax.dot_general(a, b, (((0,), (0,)), ((), ())), preferred_element_type=F32)


def add_gram(acc, slot, v):
    c = [slice(256 * j, 256 * (j + 1)) for j in range(4)]
    acc[slot, 0, :, 0:1024] += rows_dot(v[:, c[0]], v)
    acc[slot, 0, :, 1024:1280] += rows_dot(v[:, c[1]], v[:, c[1]])
    acc[slot, 1, :, 0:512] += rows_dot(v[:, c[1]], v[:, 512:])
    acc[slot, 1, :, 512:1024] += rows_dot(v[:, c[2]], v[:, 512:])
    acc[slot, 1, :, 1024:1280] += rows_dot(v[:, c[3]], v[:, c[3]])


class Sems:
    def __init__(self):
        self.n = 0

    def take(self, n=1):
        i = self.n
        self.n += n
        return i


def mega_kernel(nb, x, dy, w, ainv, sinv,
                u, own_a, oth_a, own_s, oth_s, hs, zs, gs, og, oa, os_, qg, qp,
                inb, outb, wb, acc_g, acc_p, d_g, d_p, stage, ain,
                in_sem, out_sem, w_sem, loc_sem, snd, rcv, usnd, urcv):
    dev = lax.axis_index("data")
    k = dev % 2
    c = dev // 2
    cx = c % 2
    cy = c // 2
    partner = 2 * c + (1 - k)
    xn = 2 * (2 * cy + (1 - cx)) + k
    yn = 2 * (2 * (1 - cy) + cx) + k

    def rdma(src, dst, ss, rs, to):
        return pltpu.make_async_remote_copy(src_ref=src, dst_ref=dst, send_sem=ss, recv_sem=rs,
                                            device_id=(to,), device_id_type=MESH)

    def local(src, dst, i):
        return pltpu.make_async_copy(src, dst, loc_sem.at[i])

    class Job:
        def __init__(self, kind, layer, slot):
            self.o = layer
            o = layer
            self.dg = 3 - o
            self.nx = (o // 2) * 2 + (1 - o % 2)
            self.ny = (1 - o // 2) * 2 + o % 2
            if kind == "g":
                self.acc = lambda h: acc_g.at[slot, pl.ds(h * HALF, HALF)]
                self.d, self.q, self.oo = d_g.at[layer], qg.at[layer], og
                self.rows, base = HALF, 24 * 0 + layer
                self.ch = 64
            else:
                self.acc = lambda h: acc_p.at[slot, h]
                i = layer if kind == "a" else 4 + layer
                self.d, self.q, self.oo = d_p.at[i], qp.at[i], (oa if kind == "a" else os_)
                self.rows, base = PR, 4 + i
                self.ch = 32
            self.s0 = 3 * base
            self.r0 = 6 * base
            r2 = self.rows // 2
            self.a, self.b = pl.ds(0, r2), pl.ds(r2, r2)

        def d2d(self):
            return rdma(self.acc(1 - k), self.d, snd.at[self.s0], rcv.at[self.r0], partner)

        def start(self):
            self.d2d().start()

        def finish(self):
            cp = self.d2d()
            cp.wait_recv()

            def add(i, _):
                r = pl.ds(i * self.ch, self.ch)
                self.d[r] = self.d[r] + self.acc(k)[r]
                return 0
            lax.fori_loop(0, self.rows // self.ch, add, 0)
            cp.wait_send()

        def sends(self, role):
            s1, s2 = snd.at[self.s0 + 1], snd.at[self.s0 + 2]
            r = self.r0
            d, q, oo, a, b = self.d, self.q, self.oo, self.a, self.b
            if role == "dg":
                return rdma(d.at[a], q, s1, rcv.at[r + 1], xn), rdma(d.at[b], q, s2, rcv.at[r + 1], yn)
            if role == "nx":
                return (rdma(d.at[a], oo.at[0, a], s1, rcv.at[r + 2], xn),
                        rdma(d.at[b], oo.at[0, b], s2, rcv.at[r + 3], xn))
            return (rdma(d.at[b], oo.at[1, b], s1, rcv.at[r + 4], yn),
                    rdma(d.at[a], oo.at[1, a], s2, rcv.at[r + 5], yn))

        def hop1(self):
            @pl.when(c == self.dg)
            def _():
                one, two = self.sends("dg")
                one.start()
                two.start()

            @pl.when(c == self.nx)
            def _():
                self.sends("nx")[0].start()

            @pl.when(c == self.ny)
            def _():
                self.sends("ny")[0].start()

        def hop2(self):
            r2 = self.rows // 2
            st = stage.at[:, pl.ds(0, D)] if self.rows == HALF else stage.at[pl.ds(0, r2)]

            def go(role, part, off):
                self.sends("dg")[0].wait_recv()
                cp = local(self.q, st, 0)
                cp.start()
                cp.wait()

                def add(i, _):
                    r = pl.ds(off + i * self.ch, self.ch)
                    self.d[r] = self.d[r] + st[pl.ds(i * self.ch, self.ch)]
                    return 0
                lax.fori_loop(0, r2 // self.ch, add, 0)
                self.sends(role)[1].start()

            @pl.when(c == self.nx)
            def _():
                go("nx", self.b, r2)

            @pl.when(c == self.ny)
            def _():
                go("ny", self.a, 0)

        def drain(self):
            for role, chip in (("dg", self.dg), ("nx", self.nx), ("ny", self.ny)):
                @pl.when(c == chip)
                def _():
                    one, two = self.sends(role)
                    one.wait_send()
                    two.wait_send()

        def arrive(self):
            @pl.when(c == self.o)
            def _():
                for role in ("nx", "ny"):
                    one, two = self.sends(role)
                    one.wait_recv()
                    two.wait_recv()

    slots_p = {"a0": 0, "s3": 1, "a1": 2, "a2": 0, "s2": 1, "a3": 2, "s1": 0, "s0": 1}
    job = {f"g{l}": Job("g", l, (3 - l) % 2) for l in range(4)}
    for l in range(4):
        job[f"a{l}"] = Job("a", l, slots_p[f"a{l}"])
        job[f"s{l}"] = Job("s", l, slots_p[f"s{l}"])

    def ev(what, *names):
        return [functools.partial(getattr(Job, what), job[n]) for n in names]

    def load(srcs, i, slot):
        return [pltpu.make_async_copy(s.at[pl.ds(i * BK, BK)], inb.at[j, slot], in_sem.at[j, slot])
                for j, s in enumerate(srcs)]

    def phase(srcs, dsts, body, hooks, zero, nxt, w_next=None):
        def step(i, _):
            slot = i % 2

            @pl.when(i + 1 < nb)
            def _():
                for cp in load(srcs, i + 1, 1 - slot):
                    cp.start()
            if nxt is not None:
                @pl.when(i + 1 == nb)
                def _():
                    for cp in load(nxt, 0, 1 - slot):
                        cp.start()
            for cp in load(srcs, i, slot):
                cp.wait()

            def store(i):
                return [pltpu.make_async_copy(outb.at[j, slot], t.at[pl.ds(i * BK, BK)], out_sem.at[j, slot])
                        for j, t in enumerate(dsts)]
            if dsts:
                @pl.when(i >= 2)
                def _():
                    for cp in store(i - 2):
                        cp.wait()

            @pl.when(i == 0)
            def _():
                for z in zero:
                    z[...] = jnp.zeros(z.shape, F32)
            for at in sorted(hooks):
                @pl.when(i == at)
                def _():
                    for f in hooks[at]:
                        f()
            body([inb.at[j, slot] for j in range(len(srcs))], [outb.at[j, slot] for j in range(len(dsts))])
            for cp in store(i):
                cp.start()
            return 0
        lax.fori_loop(0, nb, step, 0)
        for back in (2, 1):
            for j, t in enumerate(dsts):
                i = nb - back
                pltpu.make_async_copy(outb.at[j, i % 2], t.at[pl.ds(i * BK, BK)], out_sem.at[j, i % 2]).wait()

    def w_copy(l, slot):
        return pltpu.make_async_copy(w.at[l], wb.at[slot], w_sem.at[slot])

    def fwd_body(wslot, pslot, extra=None):
        def body(ins, outs):
            v = ins[0][...]
            z = jnp.dot(v, wb[wslot], preferred_element_type=F32).astype(BF16)
            outs[0][...] = z
            add_gram(acc_p, pslot, v)
            if extra is not None:
                add_gram(acc_p, extra, ins[1][...])
            outs[1][...] = gelu(z.astype(F32)).astype(BF16)
        return body

    def bwd_body(wslot, gslot, pslot=None):
        def body(ins, outs):
            g = ins[0][...]
            d = lax.dot_general(g, wb[wslot], (((1,), (1,)), ((), ())), preferred_element_type=F32).astype(BF16)
            acc_g[gslot] += rows_dot(ins[1][...], g)
            if pslot is not None:
                add_gram(acc_p, pslot, g)
            outs[0][...] = (d.astype(F32) * gelu_slope(ins[2][...].astype(F32))).astype(BF16)
        return body

    def cross_body(gslot):
        def body(ins, outs):
            acc_g[gslot] += rows_dot(ins[1][...], ins[0][...])
        return body

    def gram_body(*pslots):
        def body(ins, outs):
            for j, p in enumerate(pslots):
                add_gram(acc_p, p, ins[j][...])
        return body

    def u_rows(l, q):
        return u.at[l, pl.ds(k * HALF + q * (HALF // 2), HALF // 2)]

    def u_src(l, q):
        return d_g.at[l, pl.ds(q * (HALF // 2), HALF // 2)]

    def owner_sends(l):
        a = [rdma(u_src(l, q), u_rows(l, q), usnd.at[l, q], urcv.at[l, q], xn) for q in (0, 1)]
        b = [rdma(u_src(l, q), u_rows(l, q), usnd.at[l, 2 + q], urcv.at[l, q], yn) for q in (1, 0)]
        p = [rdma(u_src(l, q), u_rows(l, q), usnd.at[l, 4 + q], urcv.at[l, 2 + q], partner) for q in (0, 1)]
        return a + b + p

    def t_copy():
        half = acc_g.at[0, pl.ds(k * HALF, HALF)]
        return rdma(half, half, usnd.at[4, 0], urcv.at[4, 0], partner)

    def u_stage(chips):
        for l in chips:
            job[f"g{l}"].arrive()
        cond = functools.reduce(jnp.logical_or, [c == l for l in chips])

        @pl.when(cond)
        def _():
            cps = [local(ainv, ain, 1)] + [local(og.at[j], acc_g.at[1, pl.ds(j * HALF, HALF)], 2 + j) for j in (0, 1)]
            for cp in cps:
                cp.start()
            for cp in cps:
                cp.wait()

            def add(i, _):
                r, r2 = pl.ds(i * 64, 64), pl.ds(HALF + i * 64, 64)
                d_g[c, r] = d_g[c, r] + (acc_g[1, r] + acc_g[1, r2])
                return 0
            lax.fori_loop(0, HALF // 64, add, 0)
            cp = local(sinv.at[c], acc_g.at[1], 4)
            cp.start()
            cp.wait()
            t = jnp.dot(d_g[c], acc_g[1], precision=PRECISE, preferred_element_type=F32)
            acc_g[0, pl.ds(k * HALF, HALF)] = t * (1.0 / (nb * BK * 8))
            t_copy().start()
            t_copy().wait()
            d_g[c] = jnp.dot(ain[...], acc_g[0], precision=PRECISE, preferred_element_type=F32)
            for s in owner_sends(c):
                s.start()
            local(d_g.at[c], u.at[c, pl.ds(k * HALF, HALF)], 5).start()

    def role_of(o):
        return 3 - o, (o // 2) * 2 + (1 - o % 2), (1 - o // 2) * 2 + o % 2

    def to_partner(o, q):
        return rdma(u_rows(o, q), u_rows(o, q), usnd.at[o, q], urcv.at[o, 2 + q], partner)

    def got(o, q):
        rdma(u_rows(o, q), u_rows(o, q), usnd.at[o, 4], urcv.at[o, q], partner).wait_recv()

    def relay(o, q, to):
        return rdma(u_rows(o, q), u_rows(o, q), usnd.at[o, 4], urcv.at[o, q], to)

    def fan1(o):
        dg, nx, ny = role_of(o)

        @pl.when(c == nx)
        def _():
            got(o, 0)
            relay(o, 0, yn).start()
            to_partner(o, 0).start()

        @pl.when(c == ny)
        def _():
            got(o, 1)
            relay(o, 1, xn).start()
            to_partner(o, 1).start()

    def fan2(o):
        dg, nx, ny = role_of(o)

        @pl.when(c == nx)
        def _():
            got(o, 1)
            to_partner(o, 1).start()

        @pl.when(c == ny)
        def _():
            got(o, 0)
            to_partner(o, 0).start()

        @pl.when(c == dg)
        def _():
            for q in (0, 1):
                got(o, q)
                to_partner(o, q).start()

    def fan3(o):
        dg, nx, ny = role_of(o)

        @pl.when(c == nx)
        def _():
            relay(o, 0, yn).wait_send()

        @pl.when(c == ny)
        def _():
            relay(o, 1, xn).wait_send()

        @pl.when(c != o)
        def _():
            for q in (0, 1):
                to_partner(o, q).wait_send()

        @pl.when(c == o)
        def _():
            for s in owner_sends(o):
                s.wait_send()
            local(d_g.at[o], u.at[o, pl.ds(k * HALF, HALF)], 5).wait()
        for q in (0, 1):
            to_partner(o, q).wait_recv()

    ap = [acc_p.at[i] for i in range(3)]
    ag = [acc_g.at[i] for i in range(2)]
    h = [x, hs.at[0], hs.at[1], hs.at[2]]
    g = [gs.at[0], gs.at[1], gs.at[2], dy]
    s_f1, s_f2, s_f3 = [h[0], dy], [h[1]], [h[2]]
    s_b4, s_b3, s_b2 = [g[3], h[3], zs.at[2]], [g[2], h[2], zs.at[1]], [g[1], h[1], zs.at[0]]
    s_l1 = [g[0], h[0]]
    s_l2, s_l3 = [h[3]], [g[1], g[0]]

    w_copy(0, 0).start()
    for cp in load(s_f1, 0, 0):
        cp.start()
    w_copy(0, 0).wait()
    w_copy(1, 1).start()
    phase(s_f1, [zs.at[0], hs.at[0]], fwd_body(0, 0, 1), {}, [ap[0], ap[1]], s_f2)
    w_copy(1, 1).wait()
    w_copy(2, 0).start()
    phase(s_f2, [zs.at[1], hs.at[1]], fwd_body(1, 2),
          {0: ev("start", "a0", "s3"), 1: ev("finish", "a0", "s3") + ev("hop1", "a0", "s3"),
           6: ev("hop2", "a0", "s3")}, [ap[2]], s_f3)
    w_copy(2, 0).wait()
    w_copy(3, 1).start()
    phase(s_f3, [zs.at[2], hs.at[2]], fwd_body(0, 0),
          {0: ev("start", "a1"), 1: ev("finish", "a1") + ev("hop1", "a1"), 6: ev("hop2", "a1")}, [ap[0]], s_b4)
    w_copy(3, 1).wait()
    w_copy(2, 0).start()
    phase(s_b4, [gs.at[2]], bwd_body(1, 0),
          {0: ev("start", "a2"), 1: ev("finish", "a2") + ev("hop1", "a2"), 5: ev("hop2", "a2")}, [ag[0]], s_b3)
    w_copy(2, 0).wait()
    w_copy(1, 1).start()
    phase(s_b3, [gs.at[1]], bwd_body(0, 1, 1),
          {0: ev("start", "g3"), 1: ev("finish", "g3") + ev("hop1", "g3"),
           7: ev("hop2", "g3")}, [ag[1], ap[1]], s_b2)
    w_copy(1, 1).wait()
    phase(s_b2, [gs.at[0]], bwd_body(1, 0),
          {0: ev("start", "g2", "s2"), 1: ev("finish", "g2", "s2") + ev("hop1", "g2", "s2"),
           7: ev("hop2", "g2", "s2")}, [ag[0]], s_l1)
    phase(s_l1, [], cross_body(1),
          {0: ev("start", "g1"), 2: ev("finish", "g1") + ev("hop1", "g1")}, [ag[1]], s_l2)
    for f in ev("start", "g0") + ev("finish", "g0") + ev("hop1", "g0"):
        f()
    u_stage((3, 2))
    phase(s_l2, [], gram_body(2), {}, [ap[2]], s_l3)
    for f in ev("start", "a3") + ev("hop2", "g1", "g0"):
        f()
    phase(s_l3, [], gram_body(0, 1), {1: ev("finish", "a3") + ev("hop1", "a3")}, [ap[0], ap[1]], None)
    for f in ev("start", "s1", "s0") + ev("finish", "s1", "s0") + ev("hop1", "s1", "s0"):
        f()
    for o in (3, 2):
        fan1(o)
    for f in ev("hop2", "a3"):
        f()
    u_stage((1, 0))
    for f in ev("hop2", "s1", "s0"):
        f()
    for o in (3, 2):
        fan2(o)
    for n in ("a0", "a1", "a2", "a3", "s3", "s2", "s1", "s0", "g3", "g2", "g1", "g0"):
        job[n].drain()
        if n[0] != "g":
            job[n].arrive()

    fin = []
    for j, (src, mine, other) in enumerate(((oa, own_a, oth_a), (os_, own_s, oth_s))):
        local(src, acc_p.at[j], 6 + j).start()
    for j, (src, mine, other) in enumerate(((oa, own_a, oth_a), (os_, own_s, oth_s))):
        local(src, acc_p.at[j], 6 + j).wait()

        def add(i, _):
            r = pl.ds(i * 32, 32)
            d_p[4 * j + c, r] = d_p[4 * j + c, r] + (acc_p[j, 0, r] + acc_p[j, 1, r])
            return 0
        lax.fori_loop(0, PR // 32, add, 0)
        own = d_p.at[4 * j + c]
        fin.append((rdma(own, other, usnd.at[4, 1 + j], urcv.at[4, 1 + j], partner), local(own, mine, 8 + j)))
    for r, cp in fin:
        r.start()
        cp.start()
    for o in (1, 0):
        fan1(o)
    for o in (1, 0):
        fan2(o)
    for o in range(4):
        fan3(o)
    for r, cp in fin:
        r.wait()
        cp.wait()


def mega(x, dy, w, ainv, sinv):
    n = x.shape[0]
    nb = n // BK
    hbm = pl.BlockSpec(memory_space=pltpu.HBM)

    def sh(s, t=F32):
        return jax.ShapeDtypeStruct(s, t)
    half = (PR, PC)
    outs = [sh((4, D, D)), sh(half), sh(half), sh(half), sh(half),
            sh((3, n, D), BF16), sh((3, n, D), BF16), sh((3, n, D), BF16),
            sh((2, HALF, D)), sh((2,) + half), sh((2,) + half), sh((4, HALF // 2, D)), sh((8, PR // 2, PC))]
    dma = pltpu.SemaphoreType.DMA
    return pl.pallas_call(
        functools.partial(mega_kernel, nb),
        out_shape=outs,
        in_specs=[hbm] * 5,
        out_specs=[hbm] * len(outs),
        scratch_shapes=[
            pltpu.VMEM((3, 2, BK, D), BF16), pltpu.VMEM((2, 2, BK, D), BF16), pltpu.VMEM((2, D, D), BF16),
            pltpu.VMEM((2, D, D), F32), pltpu.VMEM((3, 2) + half, F32),
            pltpu.VMEM((4, HALF, D), F32), pltpu.VMEM((8,) + half, F32), pltpu.VMEM((HALF // 2, PC), F32),
            pltpu.VMEM((HALF, D), F32),
            dma((3, 2)), dma((2, 2)), dma((2,)), dma((10,)), dma((36,)), dma((72,)), dma((5, 6)), dma((5, 4)),
        ],
        compiler_params=pltpu.CompilerParams(has_side_effects=True, vmem_limit_bytes=66_000_000),
        name="kfac",
    )(x, dy, w, ainv, sinv)


def finish_kernel(ka, oa, ob, os_, ot, a_old, s_old, a_new, s_new):
    scale = (1.0 - FACTOR_DECAY) / (8 * 4096)

    def blend(old, new, r, cs, v):
        new[r, cs] = FACTOR_DECAY * old[r, cs] + scale * v
    c = [slice(256 * j, 256 * (j + 1)) for j in range(5)]
    for own, oth, old, new in ((oa, ob, a_old, a_new), (os_, ot, s_old, s_new)):
        @pl.when(ka[0] == 0)
        def _():
            blend(old, new, c[0], slice(0, 1024), own[:, 0:1024])
            blend(old, new, c[1], c[0], own[:, c[1]].T)
            blend(old, new, c[1], c[1], own[:, c[4]])
            blend(old, new, c[1], slice(512, 1024), oth[:, 0:512])

        @pl.when(ka[0] == 1)
        def _():
            blend(old, new, c[0], c[0], oth[:, c[2]].T)
            blend(old, new, c[0], c[1], own[:, c[0]].T)
            blend(old, new, c[0], slice(512, 1024), own[:, 512:1024])
            blend(old, new, c[1], c[0], oth[:, c[3]].T)
            blend(old, new, c[1], c[1], own[:, c[1]].T)
            blend(old, new, c[1], c[2], own[:, c[3]].T)
            blend(old, new, c[1], c[3], own[:, c[4]])


def finish(core, oa, ob, os_, ot, a_old, s_old):
    sd = jax.ShapeDtypeStruct((HALF, D), F32)
    return pl.pallas_call(
        finish_kernel,
        out_shape=[sd, sd],
        in_specs=[pl.BlockSpec(memory_space=pltpu.SMEM)] + [pl.BlockSpec(memory_space=pltpu.VMEM)] * 6,
        out_specs=[pl.BlockSpec(memory_space=pltpu.VMEM)] * 2,
        compiler_params=pltpu.CompilerParams(vmem_limit_bytes=40 * 2**20),
        name="blend",
    )(core, oa, ob, os_, ot, a_old, s_old)


def solution(mesh):
    def device_step(x_loc, dy_loc, weights, a_old_rows, s_old_rows, a_inv_rows, s_inv):
        res = mega(x_loc, dy_loc, weights, a_inv_rows, s_inv)
        core = (lax.axis_index("data") % 2).astype(jnp.int32).reshape(1)
        a_new, s_new = finish(core, res[1], res[2], res[3], res[4], a_old_rows, s_old_rows)
        return res[0], a_new, s_new

    row_spec = P("data", None)
    return jax.shard_map(
        device_step,
        mesh=mesh,
        in_specs=(row_spec, row_spec, P(), row_spec, row_spec, row_spec, P()),
        out_specs=(P(), row_spec, row_spec),
        check_vma=False,
    )
```

time: 735 us -> 501 us (0.68)
  the two profiles are of different devices: /device:TPU:0 before, /device:TPU:5 now
where the time goes in v1:
time: 501 us; the launch traced here: 492 us
  Pallas kernels  471 us (94%)
  local copies, waits for them, and re-layouts  20.4 us (4%)
    pallas_call x1, Pallas kernels, mega(): pl.pallas_call(functools.partial(mega_kernel, nb), out_shape=outs, in_spe...  468 us
    unnamed x13, local copies, waits for them, and re-layouts  20.4 us

profile of v1, /device:TPU:5, one launch (start us, length us, event | category | flops | bytes accessed | tf_op | source)
XLA Modules:
  0.0 492.5 jit_solution(8431917376994434410)
XLA Ops:
  0.6 468.1 %kfac.1 = (f32[4,1024,1024]{2,1,0:T(8,128)}, f32[256,1280]{1,0:T(8,128)}, f32[256,1280]{1,0:T(8,128)}, f32[256,1280]{1,0:T(8,128)}, f32[256,1280]{1,0:T(8,128)},...) custom-call(bf16[4096,1024]{1,0:T(8,128)(2,1)} %x.1, ...), custom_call_target="tpu_custom_call" | custom-call | tf_op jit(solution)/shard_map/kfac/pallas_call | solution.py:495
  468.8 0.0 copy-start
  468.8 1.6 copy-done
  470.4 0.0 copy-start.1
  470.4 1.6 copy-done.1
  471.9 0.0 copy-start.2
  471.9 1.3 copy-done.2
  473.3 0.0 copy-start.3
  473.3 1.3 copy-done.3
  474.6 0.0 copy-start.4
  474.6 1.3 copy-done.4
  475.9 0.0 copy-start.5
  475.9 1.3 copy-done.5
  477.2 3.1 blend.1
  480.3 12.0 %copy.11 = f32[4,1024,1024]{2,1,0:T(8,128)} copy(f32[4,1024,1024]{2,1,0:T(8,128)} %get-tuple-element.20) | data formatting | bytes 33554432
Async XLA Ops:
  468.8 1.6 copy-start
  470.4 1.6 copy-start.1
  471.9 1.3 copy-start.2
  473.3 1.3 copy-start.3
  474.6 1.3 copy-start.4
  475.9 1.3 copy-start.5
